TPU v7x, 32 devices: a whole 2x2x4 slice. The times are simulated.
32 devices in a mesh: dp: 4 (over z), section: 4 (over x, core), head: 2 (over y).
Axes of the slice: x: 2, y: 2, z: 4, core: 2. Of those that a mesh axis runs over, the one named last changes fastest.
Arguments:
- q_latent: bfloat16 [4, 2048, 1536], P('section', 'dp'), may hold values from -6 to 6
- kv_latent: bfloat16 [4, 2048, 576], P('section', 'dp'), may hold values from -6 to 6
- segment_ids: int32 [2048], P('dp'), may hold values from 0 to 31, never falling along the last dimension, each value on 1 to 512 neighbouring positions
- q_weight: bfloat16 [4, 1536, 12288], P('section', 'dp', 'head'), may hold values from -100 to 100
- k_weight: bfloat16 [4, 512, 8192], P('section', None, 'head'), may hold values from -0.25 to 0.25
Outputs:
- logit_ratio: float32 [4, 64], P(None, 'head')
- scaled_q: bfloat16 [4, 1536, 12288], P('section', 'dp', 'head')
- scaled_k: bfloat16 [4, 512, 8192], P('section', None, 'head')
All inputs are finite; a program needn't handle non-finite values.
Results may differ from a plain program's by a relative error of at most 0.0034.
Values may be sent and summed in bfloat16 or wider, within the bound.
A program may use at most 128 MiB of HBM per device.

v0:
```python
import functools
import jax
import jax.numpy as jnp
import numpy as np
from jax import lax
from jax.experimental import pallas as pl
from jax.experimental.pallas import tpu as pltpu
from jax.sharding import PartitionSpec as P

D_KV = 512
NOPE = 128
ROPE = 64
HEAD = NOPE + ROPE
LANES = 128
NEG = -1e30
VMEM_MIB = 44
MESH = pl.DeviceIdType.MESH

clip_threshold = 100.0
rope_base = 50000.0


def rotate(values, positions):
    half_width = values.shape[-1] // 2
    frequency = rope_base ** (-jnp.arange(half_width, dtype=jnp.float32) / half_width)
    angles = positions[:, None].astype(jnp.float32) * frequency[None, :]
    cosine = jnp.cos(angles)[:, None, :]
    sine_part = jnp.sin(angles)[:, None, :]
    lower_half = values[..., :half_width]
    upper_half = values[..., half_width:]
    return jnp.concatenate(
        [
            lower_half * cosine - upper_half * sine_part,
            upper_half * cosine + lower_half * sine_part,
        ],
        -1,
    )


def sequence_maxima(q_full, kv_rows, segments, w_key):
    length = kv_rows.shape[0]
    heads_here = w_key.shape[1] // NOPE
    q_full = q_full.reshape(length, heads_here, HEAD)
    positions = jnp.arange(length, dtype=jnp.int32)
    queries = jnp.concatenate(
        [q_full[..., :NOPE], rotate(q_full[..., NOPE:], positions)], -1
    ).astype(jnp.bfloat16)
    key_nope = jnp.dot(kv_rows[:, :D_KV], w_key, preferred_element_type=jnp.float32).astype(
        jnp.bfloat16
    )
    key_nope = key_nope.reshape(length, heads_here, NOPE)
    key_rope = jnp.broadcast_to(kv_rows[:, None, D_KV:], (length, heads_here, ROPE))
    keys_all = jnp.concatenate([key_nope, key_rope], -1)
    logits = jnp.einsum("shd,thd->hst", queries, keys_all, preferred_element_type=jnp.float32)
    logits = logits * HEAD ** (-0.5)
    allowed = (segments[:, None] == segments[None, :]) & (positions[None, :] <= positions[:, None])
    return jnp.max(jnp.where(allowed[None], logits, NEG), axis=(1, 2))


def scale_weights(own_max, q_weight, k_weight):
    factor = clip_threshold / jnp.maximum(own_max, clip_threshold)
    square_root = jnp.sqrt(factor)
    layers, heads = own_max.shape
    q_columns = jnp.concatenate(
        [
            jnp.broadcast_to(square_root[..., None], (layers, heads, NOPE)),
            jnp.broadcast_to(factor[..., None], (layers, heads, ROPE)),
        ],
        -1,
    ).reshape(layers, 1, heads * HEAD)
    k_columns = jnp.broadcast_to(square_root[..., None], (layers, heads, NOPE)).reshape(
        layers, 1, heads * NOPE
    )
    scaled_q = (q_weight.astype(jnp.float32) * q_columns).astype(jnp.bfloat16)
    scaled_k = (k_weight.astype(jnp.float32) * k_columns).astype(jnp.bfloat16)
    return scaled_q, scaled_k


def gathered_maxima(q_latent, kv_latent, segment_ids, q_weight, k_weight):
    q_full = jnp.dot(
        q_latent[0],
        lax.all_gather(q_weight[0], "dp", axis=0, tiled=True),
        preferred_element_type=jnp.float32,
    )
    own_max = sequence_maxima(q_full, kv_latent[0], segment_ids, k_weight[0])[None]
    layer_max = lax.pmax(own_max, "dp")
    return layer_max, lax.all_gather(layer_max, "section", axis=0, tiled=True)


def rope_tables(length):
    half = ROPE // 2
    frequency = np.float32(rope_base) ** (-np.arange(half, dtype=np.float32) / np.float32(half))
    angles = np.arange(length, dtype=np.float32)[:, None] * frequency[None, :].astype(np.float32)
    cosine, sine = np.cos(angles), np.sin(angles)
    zero = np.zeros_like(cosine)
    rest = np.zeros((length, ROPE), np.float32)
    low = [
        np.concatenate([cosine, cosine, rest + 1], 1),
        np.concatenate([-sine, zero, rest], 1),
        np.concatenate([zero, sine, rest], 1),
    ]
    high = [np.roll(t, ROPE, 1) for t in low]
    return np.stack(low + high).astype(np.float32)


def maxima_kernel(
    n_sec, x_hbm, kv_hbm, seg_hbm, q_hbm, k_hbm, tab_ref, out_ref,
    lat, kvt, seg, wq, wk, keys, bias, macc, tbuf,
    lat_recv, lat_send, seg_recv, seg_send, w_recv, w_send, k_recv, k_send, t_recv, t_send,
):
    n_seq, length, _ = lat.shape
    rows = q_hbm.shape[0]
    n_pair, d_q, pair = wq.shape
    group_q, group_k = n_pair * pair, wk.shape[1]
    part = length // 2

    z, sec, y = lax.axis_index("dp"), lax.axis_index("section"), lax.axis_index("head")
    c = lax.rem(sec, 2)
    half, z_low = z // 2, lax.rem(z, 2)
    base = sec - c
    primary = c == half
    core_peer = {"section": base + 1 - c}
    y_peer = {"head": 1 - y}
    z_peer = {"dp": 2 * half + 1 - z_low}
    entry = jnp.where(half == 0, 1, 2)
    me = z * n_sec + sec

    barrier = pltpu.get_barrier_semaphore()
    for step in range(1, n_seq * n_sec):
        other = lax.rem(me + step, n_seq * n_sec)
        pl.semaphore_signal(
            barrier, inc=1, device_id={"dp": other // n_sec, "section": lax.rem(other, n_sec)},
            device_id_type=MESH,
        )
    pl.semaphore_signal(barrier, inc=1, device_id=y_peer, device_id_type=MESH)

    def local(src, dst, sem):
        return pltpu.make_async_copy(src, dst, sem)

    def ready(dst, sem):
        pltpu.make_async_copy(dst, dst, sem).wait()

    def remote(src, dst, send, recv, where):
        return pltpu.make_async_remote_copy(
            src_ref=src, dst_ref=dst, send_sem=send, recv_sem=recv,
            device_id=where, device_id_type=MESH,
        )

    def slots(seq, h):
        at = pl.ds(pl.multiple_of(h * part, part), part)
        return lat.at[seq, at, :], kvt.at[seq, :, at]

    def own(h):
        at = pl.ds(pl.multiple_of(h * part, part), part)
        return x_hbm.at[at, :], kv_hbm.at[:, at]

    def send(sources, seq, h, at, where, do):
        for i, (src, dst) in enumerate(zip(sources, slots(seq, h))):
            getattr(
                remote(src, dst, lat_send.at[at, i], lat_recv.at[seq, h, i], where), do
            )()

    def ready_half(seq, h):
        for i, dst in enumerate(slots(seq, h)):
            ready(dst, lat_recv.at[seq, h, i])

    own_group = 2 * z_low + c
    peer_group = 2 * z_low + 1 - c

    def group_columns(g):
        return k_hbm.at[:, pl.ds(pl.multiple_of(g * group_k, group_k), group_k)]

    def seg_copy(step):
        return remote(
            seg_hbm, seg.at[z], seg_send.at[step], seg_recv.at[z],
            {"dp": lax.rem(z + step, n_seq)},
        )

    def own_sends(do):
        for step in range(1, n_seq):
            getattr(seg_copy(step), do)()

        @pl.when(jnp.logical_not(primary))
        def _():
            send(own(y), z, y, 0, {"dp": 3 - entry}, do)

        @pl.when(primary)
        def _():
            send(own(y), z, y, 0, z_peer, do)
            for h in range(2):
                send(own(h), z, h, 1 + h, core_peer, do)
            k_peer = remote(group_columns(peer_group), wk, k_send, k_recv, core_peer)
            getattr(k_peer, do)()

    def columns(p, j, act):
        turn_to = lax.rem(j + 2 * z_low, 4)
        z_to, c_to = 2 * c + turn_to // 2, lax.rem(turn_to, 2)
        offset = pl.multiple_of(turn_to * group_q + p * pair, LANES)
        src = q_hbm.at[:, pl.ds(offset, pair)]
        dst = wq.at[p, pl.ds(pl.multiple_of(z * rows, rows), rows), :]
        mine = (z_to == z) & (c_to == c)
        there = {"dp": z_to, "section": base + c_to}
        if act == "start":
            @pl.when(mine)
            def _():
                local(src, dst, w_recv.at[p, z]).start()

        @pl.when(jnp.logical_not(mine))
        def _():
            getattr(remote(src, dst, w_send.at[p, j], w_recv.at[p, z], there), act)()

    def send_columns(p):
        for j in range(4):
            columns(p, j, "start")

    pl.semaphore_wait(barrier, n_seq * n_sec)

    own_sends("start")
    local(seg_hbm, seg.at[z], seg_recv.at[z]).start()

    @pl.when(primary)
    def _():
        for h in range(2):
            for i, (src, dst) in enumerate(zip(own(h), slots(z, h))):
                local(src, dst, lat_recv.at[z, h, i]).start()
        local(group_columns(own_group), wk, k_recv).start()

    send_columns(0)
    send_columns(1)

    others = [2 * half + 1 - z_low, jnp.where(half == 0, 2, 1), jnp.where(half == 0, 3, 0)]
    at_entry = z == entry

    def relay_first(i, seq, do):
        if i > 0:
            @pl.when(at_entry)
            def _():
                send(slots(seq, y), seq, y, 6 + 4 * i, z_peer, do)
        send(slots(seq, y), seq, y, 5 + 4 * i, y_peer, do)
        send(slots(seq, y), seq, y, 3 + 4 * i, core_peer, do)

    def relay_second(i, seq, do):
        send(slots(seq, 1 - y), seq, 1 - y, 4 + 4 * i, core_peer, do)

    @pl.when(primary)
    def _():
        for i, seq in enumerate(others):
            ready_half(seq, y)
            relay_first(i, seq, "start")
        for i, seq in enumerate(others):
            ready_half(seq, 1 - y)
            relay_second(i, seq, "start")
        for h in range(2):
            ready_half(z, h)

    send_columns(2)
    send_columns(3)

    @pl.when(jnp.logical_not(primary))
    def _():
        for seq in range(n_seq):
            for h in range(2):
                ready_half(seq, h)

    ready(wk, k_recv)
    for seq in range(n_seq):
        ready(seg.at[seq], seg_recv.at[seq])

    macc[...] = jnp.full(macc.shape, NEG, jnp.float32)

    def seq_keys(s, carry):
        seg_row = seg[s].astype(jnp.float32)
        seg_col = jnp.broadcast_to(seg_row, (LANES, length)).T[:, :1]
        row = lax.broadcasted_iota(jnp.int32, (length, length), 0)
        col = lax.broadcasted_iota(jnp.int32, (length, length), 1)
        bias[s] = jnp.where((seg_col == seg_row) & (col <= row), 0.0, NEG)
        rope = kvt[s, D_KV:, :]
        none = jnp.zeros((ROPE, length), jnp.bfloat16)
        for p in range(n_pair):
            k2 = lax.dot_general(
                wk[:, p * 2 * NOPE:(p + 1) * 2 * NOPE], kvt[s, :D_KV, :],
                (((0,), (0,)), ((), ())), preferred_element_type=jnp.float32,
            ).astype(jnp.bfloat16)
            keys[s, p, 0, :NOPE, :] = k2[:NOPE]
            keys[s, p, 0, NOPE:HEAD, :] = rope
            keys[s, p, 0, HEAD:, :] = none
            keys[s, p, 1, :ROPE, :] = none
            keys[s, p, 1, ROPE:HEAD, :] = k2[NOPE:]
            keys[s, p, 1, HEAD:, :] = rope
        return carry

    lax.fori_loop(0, n_seq, seq_keys, 0)

    def turn(values, at):
        return (
            values * tab_ref[at]
            + pltpu.roll(values, LANES - ROPE // 2, 1) * tab_ref[at + 1]
            + pltpu.roll(values, ROPE // 2, 1) * tab_ref[at + 2]
        ).astype(jnp.bfloat16)

    def pair_logits(p, carry):
        for source in range(n_seq):
            ready(wq.at[p, pl.ds(source * rows, rows), :], w_recv.at[p, source])

        def one(s, inner):
            q2 = jnp.dot(lat[s], wq[p], preferred_element_type=jnp.float32)
            first = q2[:, :NOPE].astype(jnp.bfloat16)
            middle = turn(q2[:, NOPE:2 * NOPE], 0)
            last = turn(q2[:, 2 * NOPE:], 3)
            for e, tiles in enumerate(((first, middle), (middle, last))):
                queries = jnp.concatenate(tiles, 1)
                for block in range(2):
                    lo, hi = block * part, (block + 1) * part
                    logits = jnp.dot(
                        queries[lo:hi], keys[s, p, e, :, :hi], preferred_element_type=jnp.float32
                    ) + bias[s, lo:hi, :hi]
                    top = jnp.max(logits.reshape(part // 8, 8, hi), axis=0)
                    macc[2 * p + e, :, :hi] = jnp.maximum(macc[2 * p + e, :, :hi], top)
            return inner

        return lax.fori_loop(0, n_seq, one, carry)

    lax.fori_loop(0, n_pair, pair_logits, 0)

    top = jnp.max(jnp.max(macc[...], axis=1), axis=1, keepdims=True) * HEAD ** (-0.5)
    tile = jnp.broadcast_to(top, tbuf.shape)
    tbuf[...] = tile
    out_ref[me] = tile

    for p in range(n_pair):
        for j in range(4):
            columns(p, j, "wait_send")
    own_sends("wait_send")

    @pl.when(primary)
    def _():
        for i, seq in enumerate(others):
            relay_first(i, seq, "wait_send")
            relay_second(i, seq, "wait_send")

    def table_copy(step):
        other = lax.rem(me + step, n_seq * n_sec)
        return remote(
            tbuf, out_ref.at[me], t_send.at[step], t_recv.at[me],
            {"dp": other // n_sec, "section": lax.rem(other, n_sec)},
        )

    for step in range(1, n_seq * n_sec):
        table_copy(step).start()
    for step in range(1, n_seq * n_sec):
        source = lax.rem(me + step, n_seq * n_sec)
        ready(out_ref.at[source], t_recv.at[source])
    for step in range(1, n_seq * n_sec):
        table_copy(step).wait_send()


def scale_kernel(n_sec, table, q_ref, k_ref, ratio_ref, q_out, k_out):
    n_group = pl.num_programs(0)
    g = pl.program_id(0)
    sec = lax.axis_index("section")
    group = table.shape[1]

    def slot(layer, number):
        z_of = 2 * lax.rem(layer, 2) + number // 2
        return z_of * n_sec + 2 * (layer // 2) + lax.rem(number, 2)

    factor = clip_threshold / jnp.maximum(table[slot(sec, g)], clip_threshold)
    root = jnp.sqrt(factor)
    low = lax.broadcasted_iota(jnp.int32, (1, LANES), 1) < ROPE
    for p in range(group // 2):
        f_a, f_b = factor[2 * p:2 * p + 1], factor[2 * p + 1:2 * p + 2]
        r_a, r_b = root[2 * p:2 * p + 1], root[2 * p + 1:2 * p + 2]
        scales = (r_a, jnp.where(low, f_a, r_b), jnp.where(low, r_b, f_b))
        for i, scale in enumerate(scales):
            at = pl.ds(p * 2 * HEAD + i * LANES, LANES)
            q_out[:, at] = (q_ref[:, at].astype(jnp.float32) * scale).astype(jnp.bfloat16)
        for i, scale in enumerate((r_a, r_b)):
            at = pl.ds((2 * p + i) * NOPE, NOPE)
            k_out[:, at] = (k_ref[:, at].astype(jnp.float32) * scale).astype(jnp.bfloat16)

    @pl.when(g == 0)
    def _():
        lane = lax.broadcasted_iota(jnp.int32, (group, LANES), 1)
        place = lax.broadcasted_iota(jnp.int32, (group, LANES), 0)
        for layer in range(ratio_ref.shape[0]):
            line = jnp.zeros((1, LANES), jnp.float32)
            for number in range(ratio_ref.shape[1] // group):
                z_of = 2 * (layer % 2) + number // 2
                values = table[z_of * n_sec + 2 * (layer // 2) + number % 2]
                here = lane == number * group + place
                line = line + jnp.sum(jnp.where(here, values, 0.0), axis=0, keepdims=True)
            ratio_ref[layer:layer + 1, :] = line[:, :ratio_ref.shape[1]] / clip_threshold


def exchanged(sizes, q_latent, kv_latent, segment_ids, q_weight, k_weight):
    n_dp, n_sec = sizes
    _, length, d_q = q_latent.shape
    rows = q_weight.shape[1]
    heads = k_weight.shape[2] // NOPE
    group = heads // n_dp
    n_pair = group // 2
    bf16, dma = jnp.bfloat16, pltpu.SemaphoreType.DMA
    n_all = n_dp * n_sec
    table = pl.pallas_call(
        functools.partial(maxima_kernel, n_sec),
        out_shape=jax.ShapeDtypeStruct((n_all, group, LANES), jnp.float32),
        in_specs=[pl.BlockSpec(memory_space=pltpu.HBM)] * 5
        + [pl.BlockSpec(memory_space=pltpu.VMEM)],
        out_specs=pl.BlockSpec(memory_space=pltpu.VMEM),
        scratch_shapes=[
            pltpu.VMEM((n_dp, length, d_q), bf16),
            pltpu.VMEM((n_dp, D_KV + ROPE, length), bf16),
            pltpu.VMEM((n_dp, 1, length), jnp.int32),
            pltpu.VMEM((n_pair, d_q, 2 * HEAD), bf16),
            pltpu.VMEM((D_KV, group * NOPE), bf16),
            pltpu.VMEM((n_dp, n_pair, 2, 2 * NOPE, length), bf16),
            pltpu.VMEM((n_dp, length, length), jnp.float32),
            pltpu.VMEM((group, 8, length), jnp.float32),
            pltpu.VMEM((group, LANES), jnp.float32),
            dma((n_dp, 2, 2)),
            dma((15, 2)),
            dma((n_dp,)),
            dma((n_dp,)),
            dma((n_pair, n_dp)),
            dma((n_pair, 4)),
            dma,
            dma,
            dma((n_all,)),
            dma((n_all,)),
        ],
        compiler_params=pltpu.CompilerParams(
            collective_id=0, has_side_effects=True, vmem_limit_bytes=VMEM_MIB * 1024 * 1024
        ),
        cost_estimate=pl.CostEstimate(
            flops=2 * n_dp * length * group * (HEAD * (d_q + length) + NOPE * D_KV),
            bytes_accessed=2 * rows * heads * HEAD, transcendentals=0,
        ),
        name="maxima",
    )(
        q_latent[0], kv_latent[0].T, segment_ids.reshape(1, length), q_weight[0], k_weight[0],
        jnp.asarray(rope_tables(length)),
    )
    ratio, scaled_q, scaled_k = pl.pallas_call(
        functools.partial(scale_kernel, n_sec),
        grid=(n_dp,),
        out_shape=(
            jax.ShapeDtypeStruct((n_sec, heads), jnp.float32),
            jax.ShapeDtypeStruct(q_weight.shape[1:], bf16),
            jax.ShapeDtypeStruct(k_weight.shape[1:], bf16),
        ),
        in_specs=[
            pl.BlockSpec((n_all, group, LANES), lambda g: (0, 0, 0)),
            pl.BlockSpec((rows, group * HEAD), lambda g: (0, g)),
            pl.BlockSpec((D_KV, group * NOPE), lambda g: (0, g)),
        ],
        out_specs=[
            pl.BlockSpec((n_sec, heads), lambda g: (0, 0)),
            pl.BlockSpec((rows, group * HEAD), lambda g: (0, g)),
            pl.BlockSpec((D_KV, group * NOPE), lambda g: (0, g)),
        ],
        compiler_params=pltpu.CompilerParams(
            dimension_semantics=("arbitrary",), vmem_limit_bytes=24 * 1024 * 1024
        ),
        cost_estimate=pl.CostEstimate(
            flops=rows * heads * HEAD, bytes_accessed=8 * rows * heads * HEAD, transcendentals=0
        ),
        name="scale",
    )(table, q_weight[0], k_weight[0])
    return ratio, scaled_q[None], scaled_k[None]


def per_device(sizes, q_latent, kv_latent, segment_ids, q_weight, k_weight):
    n_dp, n_sec, n_head = sizes
    heads = k_weight.shape[2] // NOPE
    length = q_latent.shape[1]
    exchange = (
        n_dp == 4 and n_sec % 2 == 0 and q_weight.shape[1] % 8 == 0 and n_head == 2 and heads == 8 * n_dp
        and length % 512 == 0 and q_latent.shape[0] == 1
    )
    args = (q_latent, kv_latent, segment_ids, q_weight, k_weight)
    if exchange:
        return exchanged((n_dp, n_sec), *args)
    own, max_table = gathered_maxima(*args)
    scaled_q, scaled_k = scale_weights(own, q_weight, k_weight)
    return max_table / clip_threshold, scaled_q, scaled_k


def solution(mesh):
    sizes = tuple(mesh.shape[axis] for axis in ("dp", "section", "head"))
    return jax.shard_map(
        functools.partial(per_device, sizes),
        mesh=mesh,
        in_specs=(
            P("section", "dp", None),
            P("section", "dp", None),
            P("dp"),
            P("section", "dp", "head"),
            P("section", None, "head"),
        ),
        out_specs=(P(None, "head"), P("section", "dp", "head"), P("section", None, "head")),
        check_vma=False,
    )
```

profile of v0, /device:TPU:0, one launch (start us, length us, event | category | flops | bytes accessed | tf_op | source)
XLA Modules:
  0.0 154.0 jit_solution(4173904107391167157)
XLA Ops:
  0.6 0.0 copy-start.1
  0.6 2.2 %copy-done.1 = bf16[1,512,4096]{2,1,0:T(8,128)(2,1)S(1)} copy-done((bf16[1,512,4096]{2,1,0:T(8,128)(2,1)S(1)}, bf16[1,512,4096]{2,1,0:T(8,128)(2,1)}, u32[]{:S(2)}) %copy-start.1) | copy-done | bytes 4194328
  2.8 0.0 copy-start.2
  2.8 1.4 copy-done.2
  4.2 0.0 copy-start.3
  4.2 1.1 copy-done.3
  5.3 0.0 copy-start.4
  5.3 0.7 copy-done.4
  6.0 0.0 copy-start.5
  6.0 1.4 copy-done.5
  7.4 0.0 copy-start
  7.4 141.6 %maxima.1.table = f32[16,8,128]{2,1,0:T(8,128)S(1)} custom-call(bf16[512,1536]{1,0:T(8,128)(2,1)S(1)} %bitcast.13, bf16[576,512]{1,0:T(8,128)(2,1)S(1)} %bitcast.14, s32[1,512]{1,0:T(1,128)S(1)} %bitcast.15, bf16[384,6144]{1,0:T(8,128)(2,1)} %bitcast.9, bf16[512,4096]{1,0:T(8,128)(2,1)S(1)} %bitcast.11, f32[6,512,128]{2,1,0:T(8,128)S(1)} %copy-done.5), custom_call_target="tpu_custom_call" | custom-call | flops 15032385536 | bytes 4718592 | tf_op jit(solution)/shard_map/maxima/pallas_call | solution.py:404
  148.9 0.0 copy-done
  149.0 5.0 %scale.1 = (f32[4,32]{1,0:T(4,128)}, bf16[384,6144]{1,0:T(8,128)(2,1)}, bf16[512,4096]{1,0:T(8,128)(2,1)}) custom-call(f32[16,8,128]{2,1,0:T(8,128)S(1)} %maxima.1.table, bf16[384,6144]{1,0:T(8,128)(2,1)S(1)} %bitcast.10, bf16[512,4096]{1,0:T(8,128)(2,1)S(1)} %bitcast.12), custom_call_target="tpu_custom_call" | custom-call | flops 2359296 | bytes 18874368 | tf_op jit(solution)/shard_map/scale/pallas_call | solution.py:443
Async XLA Ops:
  0.6 2.2 %copy-start.1 = (bf16[1,512,4096]{2,1,0:T(8,128)(2,1)S(1)}, bf16[1,512,4096]{2,1,0:T(8,128)(2,1)}, u32[]{:S(2)}) copy-start(bf16[1,512,4096]{2,1,0:T(8,128)(2,1)} %param.10) | copy-start | bytes 12582916
  2.8 1.4 copy-start.2
  4.2 1.1 copy-start.3
  5.3 0.7 copy-start.4
  6.0 1.4 copy-start.5
  7.4 141.6 %copy-start = (bf16[1,384,6144]{2,1,0:T(8,128)(2,1)S(1)}, bf16[1,384,6144]{2,1,0:T(8,128)(2,1)}, u32[]{:S(2)}) copy-start(bf16[1,384,6144]{2,1,0:T(8,128)(2,1)} %param.9) | copy-start | bytes 14155780
where the time goes:
time: 154 us
  Pallas kernels  147 us (95%)
  local copies, waits for them, and re-layouts  6.74 us (4%)
    pallas_call x1, Pallas kernels, exchanged(): pl.pallas_call(functools.partial(maxima_kernel, n_sec), out_shape=jax.Sha...  142 us
    unnamed x12, local copies, waits for them, and re-layouts  6.74 us
    pallas_call x1, Pallas kernels, exchanged(): pl.pallas_call(functools.partial(scale_kernel, n_sec), grid=(n_dp,), out_...  5.03 us

commit v1 on v0

--- a/solution.py
+++ b/solution.py
@@ -104,8 +104,8 @@
 
 
 def maxima_kernel(
-    n_sec, x_hbm, kv_hbm, seg_hbm, q_hbm, k_hbm, tab_ref, out_ref,
-    lat, kvt, seg, wq, wk, keys, bias, macc, tbuf,
+    n_sec, x_hbm, kv_hbm, seg_hbm, q_hbm, k_hbm, tab_hbm, out_ref,
+    lat, kvt, seg, wq, wk, keys, bias, macc, tbuf, qacc, tab_ref, tab_sem,
     lat_recv, lat_send, seg_recv, seg_send, w_recv, w_send, k_recv, k_send, t_recv, t_send,
 ):
     n_seq, length, _ = lat.shape
@@ -113,6 +113,9 @@
     n_pair, d_q, pair = wq.shape
     group_q, group_k = n_pair * pair, wk.shape[1]
     part = length // 2
+    last = n_pair - 1
+    third = rows // 3
+    pieces = [(p, 0, rows) for p in range(last)] + [(last, i * third, third) for i in range(3)]
 
     z, sec, y = lax.axis_index("dp"), lax.axis_index("section"), lax.axis_index("head")
     c = lax.rem(sec, 2)
@@ -192,31 +195,43 @@
             k_peer = remote(group_columns(peer_group), wk, k_send, k_recv, core_peer)
             getattr(k_peer, do)()
 
-    def columns(p, j, act):
-        turn_to = lax.rem(j + 2 * z_low, 4)
+    def columns(piece, j, act):
+        p, first_row, count = pieces[piece]
+        if p < last:
+            turn_to = lax.rem(j + 2 * z_low, 4)
+        else:
+            turn_to = 2 * (c if j < 2 else 1 - c) + lax.rem(j + z_low, 2)
         z_to, c_to = 2 * c + turn_to // 2, lax.rem(turn_to, 2)
         offset = pl.multiple_of(turn_to * group_q + p * pair, LANES)
-        src = q_hbm.at[:, pl.ds(offset, pair)]
-        dst = wq.at[p, pl.ds(pl.multiple_of(z * rows, rows), rows), :]
+        src = q_hbm.at[pl.ds(first_row, count), pl.ds(offset, pair)]
+        dst = wq.at[p, pl.ds(pl.multiple_of(z * rows + first_row, third), count), :]
         mine = (z_to == z) & (c_to == c)
         there = {"dp": z_to, "section": base + c_to}
         if act == "start":
             @pl.when(mine)
             def _():
-                local(src, dst, w_recv.at[p, z]).start()
+                local(src, dst, w_recv.at[piece, z]).start()
 
         @pl.when(jnp.logical_not(mine))
         def _():
-            getattr(remote(src, dst, w_send.at[p, j], w_recv.at[p, z], there), act)()
+            getattr(remote(src, dst, w_send.at[piece, j], w_recv.at[piece, z], there), act)()
 
     def send_columns(p):
         for j in range(4):
-            columns(p, j, "start")
+            for piece in range(len(pieces)):
+                if pieces[piece][0] == p:
+                    columns(piece, j, "start")
+
+    def wait_rows(piece, source):
+        p, first_row, count = pieces[piece]
+        at = pl.ds(pl.multiple_of(source * rows + first_row, third), count)
+        ready(wq.at[p, at, :], w_recv.at[piece, source])
 
     pl.semaphore_wait(barrier, n_seq * n_sec)
 
     own_sends("start")
     local(seg_hbm, seg.at[z], seg_recv.at[z]).start()
+    local(tab_hbm, tab_ref, tab_sem).start()
 
     @pl.when(primary)
     def _():
@@ -263,6 +278,7 @@
                 ready_half(seq, h)
 
     ready(wk, k_recv)
+    ready(tab_ref, tab_sem)
     for seq in range(n_seq):
         ready(seg.at[seq], seg_recv.at[seq])
 
@@ -298,45 +314,75 @@
             + pltpu.roll(values, ROPE // 2, 1) * tab_ref[at + 2]
         ).astype(jnp.bfloat16)
 
+    def pair_maxima(p, s, q2):
+        first = q2[:, :NOPE].astype(jnp.bfloat16)
+        middle = turn(q2[:, NOPE:2 * NOPE], 0)
+        final = turn(q2[:, 2 * NOPE:], 3)
+        for e, tiles in enumerate(((first, middle), (middle, final))):
+            queries = jnp.concatenate(tiles, 1)
+            for block in range(2):
+                lo, hi = block * part, (block + 1) * part
+                logits = jnp.dot(
+                    queries[lo:hi], keys[s, p, e, :, :hi], preferred_element_type=jnp.float32
+                ) + bias[s, lo:hi, :hi]
+                top = jnp.max(logits.reshape(part // 8, 8, hi), axis=0)
+                macc[2 * p + e, :, :hi] = jnp.maximum(macc[2 * p + e, :, :hi], top)
+
     def pair_logits(p, carry):
         for source in range(n_seq):
-            ready(wq.at[p, pl.ds(source * rows, rows), :], w_recv.at[p, source])
+            at = pl.ds(source * rows, rows)
+            ready(wq.at[p, at, :], w_recv.at[p, source])
 
         def one(s, inner):
-            q2 = jnp.dot(lat[s], wq[p], preferred_element_type=jnp.float32)
-            first = q2[:, :NOPE].astype(jnp.bfloat16)
-            middle = turn(q2[:, NOPE:2 * NOPE], 0)
-            last = turn(q2[:, 2 * NOPE:], 3)
-            for e, tiles in enumerate(((first, middle), (middle, last))):
-                queries = jnp.concatenate(tiles, 1)
-                for block in range(2):
-                    lo, hi = block * part, (block + 1) * part
-                    logits = jnp.dot(
-                        queries[lo:hi], keys[s, p, e, :, :hi], preferred_element_type=jnp.float32
-                    ) + bias[s, lo:hi, :hi]
-                    top = jnp.max(logits.reshape(part // 8, 8, hi), axis=0)
-                    macc[2 * p + e, :, :hi] = jnp.maximum(macc[2 * p + e, :, :hi], top)
+            pair_maxima(p, s, jnp.dot(lat[s], wq[p], preferred_element_type=jnp.float32))
             return inner
 
         return lax.fori_loop(0, n_seq, one, carry)
 
-    lax.fori_loop(0, n_pair, pair_logits, 0)
+    lax.fori_loop(0, last, pair_logits, 0)
+
+    def partial(s, start, count):
+        at = pl.ds(pl.multiple_of(start, third), count)
+        return jnp.dot(lat[s, :, at], wq[last, at, :], preferred_element_type=jnp.float32)
+
+    near_rows = half * 2 * rows
+    far_rows = (2 * (1 - half) + c) * rows
+    final_source = 2 * (1 - half) + 1 - c
+    final_rows = final_source * rows
+
+    def from_near(s, carry):
+        qacc[s] = partial(s, near_rows, 2 * rows)
+        return carry
+
+    def from_far(s, carry):
+        qacc[s] = qacc[s] + partial(s, far_rows, rows)
+        return carry
+
+    def from_final(s, carry):
+        qacc[s] = qacc[s] + partial(s, final_rows, 2 * third)
+        return carry
+
+    def finish(s, carry):
+        pair_maxima(last, s, qacc[s] + partial(s, final_rows + 2 * third, third))
+        return carry
+
+    for z_of in range(2):
+        for piece in range(last, len(pieces)):
+            wait_rows(piece, 2 * half + z_of)
+    lax.fori_loop(0, n_seq, from_near, 0)
+    for piece in range(last, len(pieces)):
+        wait_rows(piece, 2 * (1 - half) + c)
+    lax.fori_loop(0, n_seq, from_far, 0)
+    for piece in range(last, last + 2):
+        wait_rows(piece, final_source)
+    lax.fori_loop(0, n_seq, from_final, 0)
+    wait_rows(last + 2, final_source)
+    lax.fori_loop(0, n_seq, finish, 0)
 
     top = jnp.max(jnp.max(macc[...], axis=1), axis=1, keepdims=True) * HEAD ** (-0.5)
     tile = jnp.broadcast_to(top, tbuf.shape)
     tbuf[...] = tile
     out_ref[me] = tile
-
-    for p in range(n_pair):
-        for j in range(4):
-            columns(p, j, "wait_send")
-    own_sends("wait_send")
-
-    @pl.when(primary)
-    def _():
-        for i, seq in enumerate(others):
-            relay_first(i, seq, "wait_send")
-            relay_second(i, seq, "wait_send")
 
     def table_copy(step):
         other = lax.rem(me + step, n_seq * n_sec)
@@ -347,6 +393,17 @@
 
     for step in range(1, n_seq * n_sec):
         table_copy(step).start()
+    for piece in range(len(pieces)):
+        for j in range(4):
+            columns(piece, j, "wait_send")
+    own_sends("wait_send")
+
+    @pl.when(primary)
+    def _():
+        for i, seq in enumerate(others):
+            relay_first(i, seq, "wait_send")
+            relay_second(i, seq, "wait_send")
+
     for step in range(1, n_seq * n_sec):
         source = lax.rem(me + step, n_seq * n_sec)
         ready(out_ref.at[source], t_recv.at[source])
@@ -354,42 +411,64 @@
         table_copy(step).wait_send()
 
 
-def scale_kernel(n_sec, table, q_ref, k_ref, ratio_ref, q_out, k_out):
-    n_group = pl.num_programs(0)
-    g = pl.program_id(0)
+def scale_kernel(
+    n_sec, table, q_ref, k_ref, ratio_ref, q_out, k_out, q_buf, k_buf, q_row, k_row, q_sem, k_sem
+):
+    group = table.shape[1]
+    n_group, n_pair = q_ref.shape[1] // (group * HEAD), group // 2
+    n_chunk = q_sem.shape[0]
     sec = lax.axis_index("section")
-    group = table.shape[1]
+    low = lax.broadcasted_iota(jnp.int32, (1, LANES), 1) < ROPE
 
     def slot(layer, number):
-        z_of = 2 * lax.rem(layer, 2) + number // 2
-        return z_of * n_sec + 2 * (layer // 2) + lax.rem(number, 2)
-
-    factor = clip_threshold / jnp.maximum(table[slot(sec, g)], clip_threshold)
-    root = jnp.sqrt(factor)
-    low = lax.broadcasted_iota(jnp.int32, (1, LANES), 1) < ROPE
-    for p in range(group // 2):
-        f_a, f_b = factor[2 * p:2 * p + 1], factor[2 * p + 1:2 * p + 2]
-        r_a, r_b = root[2 * p:2 * p + 1], root[2 * p + 1:2 * p + 2]
-        scales = (r_a, jnp.where(low, f_a, r_b), jnp.where(low, r_b, f_b))
-        for i, scale in enumerate(scales):
-            at = pl.ds(p * 2 * HEAD + i * LANES, LANES)
-            q_out[:, at] = (q_ref[:, at].astype(jnp.float32) * scale).astype(jnp.bfloat16)
-        for i, scale in enumerate((r_a, r_b)):
-            at = pl.ds((2 * p + i) * NOPE, NOPE)
-            k_out[:, at] = (k_ref[:, at].astype(jnp.float32) * scale).astype(jnp.bfloat16)
-
-    @pl.when(g == 0)
-    def _():
-        lane = lax.broadcasted_iota(jnp.int32, (group, LANES), 1)
-        place = lax.broadcasted_iota(jnp.int32, (group, LANES), 0)
-        for layer in range(ratio_ref.shape[0]):
-            line = jnp.zeros((1, LANES), jnp.float32)
-            for number in range(ratio_ref.shape[1] // group):
-                z_of = 2 * (layer % 2) + number // 2
-                values = table[z_of * n_sec + 2 * (layer // 2) + number % 2]
-                here = lane == number * group + place
-                line = line + jnp.sum(jnp.where(here, values, 0.0), axis=0, keepdims=True)
-            ratio_ref[layer:layer + 1, :] = line[:, :ratio_ref.shape[1]] / clip_threshold
+        z_of = 2 * (layer % 2) + number // 2
+        return z_of * n_sec + 2 * (layer // 2) + number % 2
+
+    for g in range(n_group):
+        factor = clip_threshold / jnp.maximum(table[slot(sec, g)], clip_threshold)
+        root = jnp.sqrt(factor)
+        for p in range(n_pair):
+            f_a, f_b = factor[2 * p:2 * p + 1], factor[2 * p + 1:2 * p + 2]
+            r_a, r_b = root[2 * p:2 * p + 1], root[2 * p + 1:2 * p + 2]
+            number = g * n_pair + p
+            scales = (r_a, jnp.where(low, f_a, r_b), jnp.where(low, r_b, f_b))
+            for i, scale in enumerate(scales):
+                q_row[:, pl.ds((3 * number + i) * LANES, LANES)] = scale
+            for i, scale in enumerate((r_a, r_b)):
+                k_row[:, pl.ds((2 * number + i) * LANES, LANES)] = scale
+
+    def block(source, target, sem, i):
+        count = source.shape[0] // n_chunk
+        at = pl.ds(pl.multiple_of(i * count, count), count)
+        return at, pltpu.make_async_copy(source.at[at, :], target.at[at, :], sem.at[i])
+
+    def one_chunk(i, carry):
+        for source, row, buf, target, sem in (
+            (q_ref, q_row, q_buf, q_out, q_sem), (k_ref, k_row, k_buf, k_out, k_sem),
+        ):
+            at, copy = block(buf, target, sem, i)
+            for tile in range(source.shape[1] // LANES):
+                lanes = pl.ds(tile * LANES, LANES)
+                values = source[at, lanes].astype(jnp.float32) * row[:, lanes]
+                buf[at, lanes] = values.astype(jnp.bfloat16)
+            copy.start()
+        return carry
+
+    lax.fori_loop(0, n_chunk, one_chunk, 0)
+
+    lane = lax.broadcasted_iota(jnp.int32, (group, LANES), 1)
+    place = lax.broadcasted_iota(jnp.int32, (group, LANES), 0)
+    for layer in range(ratio_ref.shape[0]):
+        line = jnp.zeros((1, LANES), jnp.float32)
+        for number in range(n_group):
+            values = table[slot(layer, number)]
+            here = lane == number * group + place
+            line = line + jnp.sum(jnp.where(here, values, 0.0), axis=0, keepdims=True)
+        ratio_ref[layer:layer + 1, :] = line[:, :ratio_ref.shape[1]] / clip_threshold
+
+    for i in range(n_chunk):
+        block(q_buf, q_out, q_sem, i)[1].wait()
+        block(k_buf, k_out, k_sem, i)[1].wait()
 
 
 def exchanged(sizes, q_latent, kv_latent, segment_ids, q_weight, k_weight):
@@ -404,8 +483,7 @@
     table = pl.pallas_call(
         functools.partial(maxima_kernel, n_sec),
         out_shape=jax.ShapeDtypeStruct((n_all, group, LANES), jnp.float32),
-        in_specs=[pl.BlockSpec(memory_space=pltpu.HBM)] * 5
-        + [pl.BlockSpec(memory_space=pltpu.VMEM)],
+        in_specs=[pl.BlockSpec(memory_space=pltpu.HBM)] * 6,
         out_specs=pl.BlockSpec(memory_space=pltpu.VMEM),
         scratch_shapes=[
             pltpu.VMEM((n_dp, length, d_q), bf16),
@@ -417,12 +495,15 @@
             pltpu.VMEM((n_dp, length, length), jnp.float32),
             pltpu.VMEM((group, 8, length), jnp.float32),
             pltpu.VMEM((group, LANES), jnp.float32),
+            pltpu.VMEM((n_dp, length, 2 * HEAD), jnp.float32),
+            pltpu.VMEM((6, length, LANES), jnp.float32),
+            dma,
             dma((n_dp, 2, 2)),
             dma((15, 2)),
             dma((n_dp,)),
             dma((n_dp,)),
-            dma((n_pair, n_dp)),
-            dma((n_pair, 4)),
+            dma((n_pair + 2, n_dp)),
+            dma((n_pair + 2, 4)),
             dma,
             dma,
             dma((n_all,)),
@@ -437,30 +518,33 @@
         ),
         name="maxima",
     )(
-        q_latent[0], kv_latent[0].T, segment_ids.reshape(1, length), q_weight[0], k_weight[0],
-        jnp.asarray(rope_tables(length)),
+        *[
+            pltpu.with_memory_space_constraint(a, pltpu.HBM)
+            for a in (
+                q_latent[0], kv_latent[0].T, segment_ids.reshape(1, length), q_weight[0],
+                k_weight[0], jnp.asarray(rope_tables(length)),
+            )
+        ],
     )
     ratio, scaled_q, scaled_k = pl.pallas_call(
         functools.partial(scale_kernel, n_sec),
-        grid=(n_dp,),
         out_shape=(
             jax.ShapeDtypeStruct((n_sec, heads), jnp.float32),
             jax.ShapeDtypeStruct(q_weight.shape[1:], bf16),
             jax.ShapeDtypeStruct(k_weight.shape[1:], bf16),
         ),
-        in_specs=[
-            pl.BlockSpec((n_all, group, LANES), lambda g: (0, 0, 0)),
-            pl.BlockSpec((rows, group * HEAD), lambda g: (0, g)),
-            pl.BlockSpec((D_KV, group * NOPE), lambda g: (0, g)),
+        in_specs=[pl.BlockSpec(memory_space=pltpu.VMEM)] * 3,
+        out_specs=[pl.BlockSpec(memory_space=pltpu.VMEM)]
+        + [pl.BlockSpec(memory_space=pltpu.HBM)] * 2,
+        scratch_shapes=[
+            pltpu.VMEM(q_weight.shape[1:], bf16),
+            pltpu.VMEM(k_weight.shape[1:], bf16),
+            pltpu.VMEM((1, q_weight.shape[2]), jnp.float32),
+            pltpu.VMEM((1, k_weight.shape[2]), jnp.float32),
+            dma((8,)),
+            dma((8,)),
         ],
-        out_specs=[
-            pl.BlockSpec((n_sec, heads), lambda g: (0, 0)),
-            pl.BlockSpec((rows, group * HEAD), lambda g: (0, g)),
-            pl.BlockSpec((D_KV, group * NOPE), lambda g: (0, g)),
-        ],
-        compiler_params=pltpu.CompilerParams(
-            dimension_semantics=("arbitrary",), vmem_limit_bytes=24 * 1024 * 1024
-        ),
+        compiler_params=pltpu.CompilerParams(vmem_limit_bytes=24 * 1024 * 1024),
         cost_estimate=pl.CostEstimate(
             flops=rows * heads * HEAD, bytes_accessed=8 * rows * heads * HEAD, transcendentals=0
         ),
@@ -474,7 +558,7 @@
     heads = k_weight.shape[2] // NOPE
     length = q_latent.shape[1]
     exchange = (
-        n_dp == 4 and n_sec % 2 == 0 and q_weight.shape[1] % 8 == 0 and n_head == 2 and heads == 8 * n_dp
+        n_dp == 4 and n_sec % 2 == 0 and q_weight.shape[1] % 384 == 0 and n_head == 2 and heads == 8 * n_dp
         and length % 512 == 0 and q_latent.shape[0] == 1
     )
     args = (q_latent, kv_latent, segment_ids, q_weight, k_weight)

time: 154 us -> 146 us (0.948)
  local copies, waits for them, and re-layouts: 6.74 us -> 0.01 us
  Pallas kernels: 147 us -> 145 us
    unnamed x12 -> x4, local copies, waits for them, and re-layouts: 6.74 us -> 0.01 us
where the time goes in v1:
time: 146 us; the launch traced here: 145 us
  Pallas kernels  145 us (99%)
    pallas_call x1, Pallas kernels, exchanged(): pl.pallas_call(functools.partial(maxima_kernel, n_sec), out_shape=jax.Sha...  140 us
    pallas_call x1, Pallas kernels, exchanged(): pl.pallas_call(functools.partial(scale_kernel, n_sec), out_shape=(jax.Sha...  4.33 us

profile of v1, /device:TPU:0, one launch (start us, length us, event | category | flops | bytes accessed | tf_op | source)
XLA Modules:
  0.0 145.4 jit_solution(10459395075674497579)
XLA Ops:
  0.6 0.0 copy-start
  0.6 0.0 copy-start.1
  0.7 140.4 %maxima.1.table = f32[16,8,128]{2,1,0:T(8,128)S(1)} custom-call(bf16[512,1536]{1,0:T(8,128)(2,1)} %bitcast.15, bf16[576,512]{1,0:T(8,128)(2,1)} %bitcast.16, s32[1,512]{1,0:T(1,128)} %bitcast.17, bf16[384,6144]{1,0:T(8,128)(2,1)} %bitcast.9, bf16[512,4096]{1,0:T(8,128)(2,1)} %bitcast.11, f32[6,512,128]{2,1,0:T(8,128)} %constant.2.clone.tab_hbm), custom_call_target="tpu_custom_call" | custom-call | flops 15032385536 | bytes 4718592 | tf_op jit(solution)/shard_map/maxima/pallas_call | solution.py:483
  141.0 0.0 copy-done
  141.0 0.0 copy-done.1
  141.1 4.3 %scale.1 = (f32[4,32]{1,0:T(4,128)}, bf16[384,6144]{1,0:T(8,128)(2,1)}, bf16[512,4096]{1,0:T(8,128)(2,1)}) custom-call(f32[16,8,128]{2,1,0:T(8,128)S(1)} %maxima.1.table, bf16[384,6144]{1,0:T(8,128)(2,1)S(1)} %bitcast.10, bf16[512,4096]{1,0:T(8,128)(2,1)S(1)} %bitcast.12), custom_call_target="tpu_custom_call" | custom-call | flops 2359296 | bytes 18874368 | tf_op jit(solution)/shard_map/scale/pallas_call | solution.py:529
Async XLA Ops:
  0.6 140.4 %copy-start = (bf16[1,384,6144]{2,1,0:T(8,128)(2,1)S(1)}, bf16[1,384,6144]{2,1,0:T(8,128)(2,1)}, u32[]{:S(2)}) copy-start(bf16[1,384,6144]{2,1,0:T(8,128)(2,1)} %param.9) | copy-start | bytes 14155780
  0.6 140.4 %copy-start.1 = (bf16[1,512,4096]{2,1,0:T(8,128)(2,1)S(1)}, bf16[1,512,4096]{2,1,0:T(8,128)(2,1)}, u32[]{:S(2)}) copy-start(bf16[1,512,4096]{2,1,0:T(8,128)(2,1)} %param.10) | copy-start | bytes 12582916

commit v2 on v1

--- a/solution.py
+++ b/solution.py
@@ -105,7 +105,7 @@
 
 def maxima_kernel(
     n_sec, x_hbm, kv_hbm, seg_hbm, q_hbm, k_hbm, tab_hbm, out_ref,
-    lat, kvt, seg, wq, wk, keys, bias, macc, tbuf, qacc, tab_ref, tab_sem,
+    lat, kvt, seg, wq, wk, keys, bias, macc, tbuf, qacc, mid, tab_ref, outer_sem, line_sem, side_sem, all_sem, tab_sem,
     lat_recv, lat_send, seg_recv, seg_send, w_recv, w_send, k_recv, k_send, t_recv, t_send,
 ):
     n_seq, length, _ = lat.shape
@@ -115,7 +115,12 @@
     part = length // 2
     last = n_pair - 1
     third = rows // 3
-    pieces = [(p, 0, rows) for p in range(last)] + [(last, i * third, third) for i in range(3)]
+    pieces = [(p, 0, rows, 0, pair) for p in range(last)]
+    pieces += [
+        (last, 0, rows, 0, 2 * LANES),
+        (last, 0, 2 * third, 2 * LANES, LANES),
+        (last, 2 * third, third, 2 * LANES, LANES),
+    ]
 
     z, sec, y = lax.axis_index("dp"), lax.axis_index("section"), lax.axis_index("head")
     c = lax.rem(sec, 2)
@@ -128,14 +133,29 @@
     entry = jnp.where(half == 0, 1, 2)
     me = z * n_sec + sec
 
+    mid_z, outer_z = 3 - z, jnp.where(half == 0, 0, 3)
+    inner = z == entry
+    outer = jnp.logical_not(inner)
+    both_cores = [base, base + 1]
+    side_peers = [{"section": lax.rem(sec + 2 * i, n_sec)} for i in range(1, n_sec // 2)]
+    side_peers.append(y_peer)
+
+    def signal(sem, where):
+        pl.semaphore_signal(sem, inc=1, device_id=where, device_id_type=MESH)
+
     barrier = pltpu.get_barrier_semaphore()
-    for step in range(1, n_seq * n_sec):
-        other = lax.rem(me + step, n_seq * n_sec)
-        pl.semaphore_signal(
-            barrier, inc=1, device_id={"dp": other // n_sec, "section": lax.rem(other, n_sec)},
-            device_id_type=MESH,
-        )
-    pl.semaphore_signal(barrier, inc=1, device_id=y_peer, device_id_type=MESH)
+
+    @pl.when(inner)
+    def _():
+        for there in both_cores:
+            signal(barrier, {"dp": mid_z, "section": there})
+        for there in both_cores:
+            signal(barrier, {"dp": outer_z, "section": there})
+
+    @pl.when(outer)
+    def _():
+        for where in side_peers:
+            signal(barrier, where)
 
     def local(src, dst, sem):
         return pltpu.make_async_copy(src, dst, sem)
@@ -179,13 +199,16 @@
             {"dp": lax.rem(z + step, n_seq)},
         )
 
+    def first_send(do):
+        send(own(y), z, y, 0, {"dp": 3 - entry}, do)
+
     def own_sends(do):
         for step in range(1, n_seq):
             getattr(seg_copy(step), do)()
 
-        @pl.when(jnp.logical_not(primary))
+        @pl.when(jnp.logical_not(primary) & (outer if do == "start" else True))
         def _():
-            send(own(y), z, y, 0, {"dp": 3 - entry}, do)
+            first_send(do)
 
         @pl.when(primary)
         def _():
@@ -195,16 +218,21 @@
             k_peer = remote(group_columns(peer_group), wk, k_send, k_recv, core_peer)
             getattr(k_peer, do)()
 
+    def rows_of(piece, source):
+        p, first_row, count, first_column, width = pieces[piece]
+        at = pl.ds(pl.multiple_of(source * rows + first_row, third), count)
+        return wq.at[p, at, pl.ds(first_column, width)]
+
     def columns(piece, j, act):
-        p, first_row, count = pieces[piece]
+        p, first_row, count, first_column, width = pieces[piece]
         if p < last:
             turn_to = lax.rem(j + 2 * z_low, 4)
         else:
-            turn_to = 2 * (c if j < 2 else 1 - c) + lax.rem(j + z_low, 2)
+            turn_to = 2 * (1 - c if j < 2 else c) + j % 2
         z_to, c_to = 2 * c + turn_to // 2, lax.rem(turn_to, 2)
-        offset = pl.multiple_of(turn_to * group_q + p * pair, LANES)
-        src = q_hbm.at[pl.ds(first_row, count), pl.ds(offset, pair)]
-        dst = wq.at[p, pl.ds(pl.multiple_of(z * rows + first_row, third), count), :]
+        offset = pl.multiple_of(turn_to * group_q + p * pair + first_column, LANES)
+        src = q_hbm.at[pl.ds(first_row, count), pl.ds(offset, width)]
+        dst = rows_of(piece, z)
         mine = (z_to == z) & (c_to == c)
         there = {"dp": z_to, "section": base + c_to}
         if act == "start":
@@ -218,16 +246,36 @@
 
     def send_columns(p):
         for j in range(4):
-            for piece in range(len(pieces)):
-                if pieces[piece][0] == p:
-                    columns(piece, j, "start")
+            columns(p, j, "start")
+
+    def send_last_columns():
+        for j in range(4):
+            columns(last, j, "start")
+        for j in (2, 3, 0, 1):
+            for piece in range(last + 1, len(pieces)):
+                columns(piece, j, "start")
 
     def wait_rows(piece, source):
-        p, first_row, count = pieces[piece]
-        at = pl.ds(pl.multiple_of(source * rows + first_row, third), count)
-        ready(wq.at[p, at, :], w_recv.at[piece, source])
-
-    pl.semaphore_wait(barrier, n_seq * n_sec)
+        ready(rows_of(piece, source), w_recv.at[piece, source])
+
+    pl.semaphore_wait(barrier, jnp.where(inner, 2, 2 + len(side_peers)))
+
+    @pl.when(inner & jnp.logical_not(primary))
+    def _():
+        first_send("start")
+
+    @pl.when(outer)
+    def _():
+        for there in both_cores:
+            signal(outer_sem, {"dp": entry, "section": there})
+        pl.semaphore_wait(line_sem, 1)
+
+    @pl.when(inner)
+    def _():
+        pl.semaphore_wait(outer_sem, 2)
+        signal(line_sem, {"dp": mid_z})
+        pl.semaphore_wait(line_sem, 1)
+        signal(line_sem, {"dp": outer_z})
 
     own_sends("start")
     local(seg_hbm, seg.at[z], seg_recv.at[z]).start()
@@ -242,6 +290,17 @@
 
     send_columns(0)
     send_columns(1)
+
+    @pl.when(outer)
+    def _():
+        for where in side_peers:
+            signal(side_sem, where)
+        pl.semaphore_wait(side_sem, len(side_peers))
+        signal(all_sem, {"dp": entry})
+
+    @pl.when(inner)
+    def _():
+        pl.semaphore_wait(all_sem, 1)
 
     others = [2 * half + 1 - z_low, jnp.where(half == 0, 2, 1), jnp.where(half == 0, 3, 0)]
     at_entry = z == entry
@@ -268,8 +327,9 @@
         for h in range(2):
             ready_half(z, h)
 
-    send_columns(2)
-    send_columns(3)
+    for p in range(2, last):
+        send_columns(p)
+    send_last_columns()
 
     @pl.when(jnp.logical_not(primary))
     def _():
@@ -314,19 +374,30 @@
             + pltpu.roll(values, ROPE // 2, 1) * tab_ref[at + 2]
         ).astype(jnp.bfloat16)
 
+    def tops(p, e, s, tiles):
+        queries = jnp.concatenate(tiles, 1)
+        found = []
+        for block in range(2):
+            lo, hi = block * part, (block + 1) * part
+            logits = jnp.dot(
+                queries[lo:hi], keys[s, p, e, :, :hi], preferred_element_type=jnp.float32
+            ) + bias[s, lo:hi, :hi]
+            found.append(jnp.max(logits.reshape(part // 8, 8, hi), axis=0))
+        return found
+
+    def keep(p, e, found):
+        for block, top in enumerate(found):
+            hi = (block + 1) * part
+            macc[2 * p + e, :, :hi] = jnp.maximum(macc[2 * p + e, :, :hi], top)
+
+    def head_maxima(p, e, s, tiles):
+        keep(p, e, tops(p, e, s, tiles))
+
     def pair_maxima(p, s, q2):
         first = q2[:, :NOPE].astype(jnp.bfloat16)
         middle = turn(q2[:, NOPE:2 * NOPE], 0)
-        final = turn(q2[:, 2 * NOPE:], 3)
-        for e, tiles in enumerate(((first, middle), (middle, final))):
-            queries = jnp.concatenate(tiles, 1)
-            for block in range(2):
-                lo, hi = block * part, (block + 1) * part
-                logits = jnp.dot(
-                    queries[lo:hi], keys[s, p, e, :, :hi], preferred_element_type=jnp.float32
-                ) + bias[s, lo:hi, :hi]
-                top = jnp.max(logits.reshape(part // 8, 8, hi), axis=0)
-                macc[2 * p + e, :, :hi] = jnp.maximum(macc[2 * p + e, :, :hi], top)
+        head_maxima(p, 0, s, (first, middle))
+        head_maxima(p, 1, s, (middle, turn(q2[:, 2 * NOPE:], 3)))
 
     def pair_logits(p, carry):
         for source in range(n_seq):
@@ -341,43 +412,55 @@
 
     lax.fori_loop(0, last, pair_logits, 0)
 
-    def partial(s, start, count):
-        at = pl.ds(pl.multiple_of(start, third), count)
-        return jnp.dot(lat[s, :, at], wq[last, at, :], preferred_element_type=jnp.float32)
-
-    near_rows = half * 2 * rows
-    far_rows = (2 * (1 - half) + c) * rows
-    final_source = 2 * (1 - half) + 1 - c
-    final_rows = final_source * rows
+    def partial(s, starts, count, first_column, width):
+        spans = [pl.ds(pl.multiple_of(start, third), count) for start in starts]
+        tokens = [lat[s, :, at] for at in spans]
+        weights = [wq[last, at, pl.ds(first_column, width)] for at in spans]
+        if len(spans) > 1:
+            tokens, weights = [jnp.concatenate(tokens, 1)], [jnp.concatenate(weights, 0)]
+        return jnp.dot(tokens[0], weights[0], preferred_element_type=jnp.float32)
+
+    near_sources = [2 * half, 2 * half + 1]
+    far_sources = [2 * (1 - half), 2 * (1 - half) + 1]
+    far_rows = [source * rows for source in far_sources]
+    whole, narrow = last, slice(2 * LANES, 3 * LANES)
 
     def from_near(s, carry):
-        qacc[s] = partial(s, near_rows, 2 * rows)
+        qacc[s] = partial(s, [near_sources[0] * rows], 2 * rows, 0, pair)
         return carry
 
     def from_far(s, carry):
-        qacc[s] = qacc[s] + partial(s, far_rows, rows)
+        q2 = qacc[s, :, :2 * LANES] + partial(s, far_rows[:1], 2 * rows, 0, 2 * LANES)
+        middle = turn(q2[:, LANES:], 0)
+        mid[s] = middle
+        head_maxima(last, 0, s, (q2[:, :LANES].astype(jnp.bfloat16), middle))
         return carry
 
-    def from_final(s, carry):
-        qacc[s] = qacc[s] + partial(s, final_rows, 2 * third)
+    def from_far_tile(s, carry):
+        qacc[s, :, narrow] = qacc[s, :, narrow] + partial(
+            s, far_rows, 2 * third, 2 * LANES, LANES
+        )
         return carry
 
-    def finish(s, carry):
-        pair_maxima(last, s, qacc[s] + partial(s, final_rows + 2 * third, third))
-        return carry
-
-    for z_of in range(2):
+    def finish(s):
+        starts = [start + 2 * third for start in far_rows]
+        q1 = qacc[s, :, narrow] + partial(s, starts, third, 2 * LANES, LANES)
+        return tops(last, 1, s, (mid[s], turn(q1, 3)))
+
+    for source in near_sources:
         for piece in range(last, len(pieces)):
-            wait_rows(piece, 2 * half + z_of)
+            wait_rows(piece, source)
     lax.fori_loop(0, n_seq, from_near, 0)
-    for piece in range(last, len(pieces)):
-        wait_rows(piece, 2 * (1 - half) + c)
+    for source in far_sources:
+        wait_rows(whole, source)
     lax.fori_loop(0, n_seq, from_far, 0)
-    for piece in range(last, last + 2):
-        wait_rows(piece, final_source)
-    lax.fori_loop(0, n_seq, from_final, 0)
-    wait_rows(last + 2, final_source)
-    lax.fori_loop(0, n_seq, finish, 0)
+    for source in far_sources:
+        wait_rows(last + 1, source)
+    lax.fori_loop(0, n_seq, from_far_tile, 0)
+    for source in far_sources:
+        wait_rows(last + 2, source)
+    found = [finish(s) for s in range(n_seq)]
+    keep(last, 1, [functools.reduce(jnp.maximum, tops_of) for tops_of in zip(*found)])
 
     top = jnp.max(jnp.max(macc[...], axis=1), axis=1, keepdims=True) * HEAD ** (-0.5)
     tile = jnp.broadcast_to(top, tbuf.shape)
@@ -496,7 +579,9 @@
             pltpu.VMEM((group, 8, length), jnp.float32),
             pltpu.VMEM((group, LANES), jnp.float32),
             pltpu.VMEM((n_dp, length, 2 * HEAD), jnp.float32),
+            pltpu.VMEM((n_dp, length, LANES), bf16),
             pltpu.VMEM((6, length, LANES), jnp.float32),
+            *[pltpu.SemaphoreType.REGULAR] * 4,
             dma,
             dma((n_dp, 2, 2)),
             dma((15, 2)),

time: 146 us -> 143 us (0.979)
  Pallas kernels: 145 us -> 142 us
    pallas_call x1, Pallas kernels: 140 us -> 138 us  [exchanged(): pl.pallas_call(functools.partial(maxima_kernel, n_sec), out_shape=jax.Sha...]
where the time goes in v2:
time: 143 us
  Pallas kernels  142 us (99%)
    pallas_call x1, Pallas kernels, exchanged(): pl.pallas_call(functools.partial(maxima_kernel, n_sec), out_shape=jax.Sha...  138 us
    pallas_call x1, Pallas kernels, exchanged(): pl.pallas_call(functools.partial(scale_kernel, n_sec), out_shape=(jax.Sha...  4.33 us

profile of v2, /device:TPU:0, one launch (start us, length us, event | category | flops | bytes accessed | tf_op | source)
XLA Modules:
  0.0 142.8 jit_solution(15164312463869639039)
XLA Ops:
  0.6 0.0 copy-start
  0.6 0.0 copy-start.1
  0.7 137.8 %maxima.1.table = f32[16,8,128]{2,1,0:T(8,128)S(1)} custom-call(bf16[512,1536]{1,0:T(8,128)(2,1)} %bitcast.15, bf16[576,512]{1,0:T(8,128)(2,1)} %bitcast.16, s32[1,512]{1,0:T(1,128)} %bitcast.17, bf16[384,6144]{1,0:T(8,128)(2,1)} %bitcast.9, bf16[512,4096]{1,0:T(8,128)(2,1)} %bitcast.11, f32[6,512,128]{2,1,0:T(8,128)} %constant.2.clone.tab_hbm), custom_call_target="tpu_custom_call" | custom-call | flops 15032385536 | bytes 4718592 | tf_op jit(solution)/shard_map/maxima/pallas_call | solution.py:566
  138.5 0.0 copy-done
  138.5 0.0 copy-done.1
  138.5 4.3 %scale.1 = (f32[4,32]{1,0:T(4,128)}, bf16[384,6144]{1,0:T(8,128)(2,1)}, bf16[512,4096]{1,0:T(8,128)(2,1)}) custom-call(f32[16,8,128]{2,1,0:T(8,128)S(1)} %maxima.1.table, bf16[384,6144]{1,0:T(8,128)(2,1)S(1)} %bitcast.10, bf16[512,4096]{1,0:T(8,128)(2,1)S(1)} %bitcast.12), custom_call_target="tpu_custom_call" | custom-call | flops 2359296 | bytes 18874368 | tf_op jit(solution)/shard_map/scale/pallas_call | solution.py:614
Async XLA Ops:
  0.6 137.9 %copy-start = (bf16[1,384,6144]{2,1,0:T(8,128)(2,1)S(1)}, bf16[1,384,6144]{2,1,0:T(8,128)(2,1)}, u32[]{:S(2)}) copy-start(bf16[1,384,6144]{2,1,0:T(8,128)(2,1)} %param.9) | copy-start | bytes 14155780
  0.6 137.9 %copy-start.1 = (bf16[1,512,4096]{2,1,0:T(8,128)(2,1)S(1)}, bf16[1,512,4096]{2,1,0:T(8,128)(2,1)}, u32[]{:S(2)}) copy-start(bf16[1,512,4096]{2,1,0:T(8,128)(2,1)} %param.10) | copy-start | bytes 12582916

commit v3 on v2

--- a/solution.py
+++ b/solution.py
@@ -92,12 +92,10 @@
     frequency = np.float32(rope_base) ** (-np.arange(half, dtype=np.float32) / np.float32(half))
     angles = np.arange(length, dtype=np.float32)[:, None] * frequency[None, :].astype(np.float32)
     cosine, sine = np.cos(angles), np.sin(angles)
-    zero = np.zeros_like(cosine)
     rest = np.zeros((length, ROPE), np.float32)
     low = [
         np.concatenate([cosine, cosine, rest + 1], 1),
-        np.concatenate([-sine, zero, rest], 1),
-        np.concatenate([zero, sine, rest], 1),
+        np.concatenate([-sine, sine, rest], 1),
     ]
     high = [np.roll(t, ROPE, 1) for t in low]
     return np.stack(low + high).astype(np.float32)
@@ -105,7 +103,7 @@
 
 def maxima_kernel(
     n_sec, x_hbm, kv_hbm, seg_hbm, q_hbm, k_hbm, tab_hbm, out_ref,
-    lat, kvt, seg, wq, wk, keys, bias, macc, tbuf, qacc, mid, tab_ref, outer_sem, line_sem, side_sem, all_sem, tab_sem,
+    lat, kvt, seg, wq, wk, keys, bias, macc, tbuf, qacc, mid, mid2, tab_ref, outer_sem, line_sem, side_sem, all_sem, tab_sem,
     lat_recv, lat_send, seg_recv, seg_send, w_recv, w_send, k_recv, k_send, t_recv, t_send,
 ):
     n_seq, length, _ = lat.shape
@@ -251,9 +249,10 @@
     def send_last_columns():
         for j in range(4):
             columns(last, j, "start")
-        for j in (2, 3, 0, 1):
+        for first in (2, 0):
             for piece in range(last + 1, len(pieces)):
-                columns(piece, j, "start")
+                for j in (first, first + 1):
+                    columns(piece, j, "start")
 
     def wait_rows(piece, source):
         ready(rows_of(piece, source), w_recv.at[piece, source])
@@ -367,12 +366,13 @@
 
     lax.fori_loop(0, n_seq, seq_keys, 0)
 
+    lower = lax.rem(lax.broadcasted_iota(jnp.int32, (1, LANES), 1), ROPE) < ROPE // 2
+
     def turn(values, at):
-        return (
-            values * tab_ref[at]
-            + pltpu.roll(values, LANES - ROPE // 2, 1) * tab_ref[at + 1]
-            + pltpu.roll(values, ROPE // 2, 1) * tab_ref[at + 2]
-        ).astype(jnp.bfloat16)
+        swapped = jnp.where(
+            lower, pltpu.roll(values, LANES - ROPE // 2, 1), pltpu.roll(values, ROPE // 2, 1)
+        )
+        return (values * tab_ref[at] + swapped * tab_ref[at + 1]).astype(jnp.bfloat16)
 
     def tops(p, e, s, tiles):
         queries = jnp.concatenate(tiles, 1)
@@ -380,15 +380,15 @@
         for block in range(2):
             lo, hi = block * part, (block + 1) * part
             logits = jnp.dot(
-                queries[lo:hi], keys[s, p, e, :, :hi], preferred_element_type=jnp.float32
-            ) + bias[s, lo:hi, :hi]
-            found.append(jnp.max(logits.reshape(part // 8, 8, hi), axis=0))
+                queries[lo:, :], keys[s, p, e, :, lo:hi], preferred_element_type=jnp.float32
+            ) + bias[s, lo:, lo:hi]
+            found.append(jnp.max(logits.reshape((length - lo) // 8, 8, part), axis=0))
         return found
 
     def keep(p, e, found):
         for block, top in enumerate(found):
-            hi = (block + 1) * part
-            macc[2 * p + e, :, :hi] = jnp.maximum(macc[2 * p + e, :, :hi], top)
+            at = slice(block * part, (block + 1) * part)
+            macc[2 * p + e, :, at] = jnp.maximum(macc[2 * p + e, :, at], top)
 
     def head_maxima(p, e, s, tiles):
         keep(p, e, tops(p, e, s, tiles))
@@ -397,7 +397,7 @@
         first = q2[:, :NOPE].astype(jnp.bfloat16)
         middle = turn(q2[:, NOPE:2 * NOPE], 0)
         head_maxima(p, 0, s, (first, middle))
-        head_maxima(p, 1, s, (middle, turn(q2[:, 2 * NOPE:], 3)))
+        head_maxima(p, 1, s, (middle, turn(q2[:, 2 * NOPE:], 2)))
 
     def pair_logits(p, carry):
         for source in range(n_seq):
@@ -445,7 +445,7 @@
     def finish(s):
         starts = [start + 2 * third for start in far_rows]
         q1 = qacc[s, :, narrow] + partial(s, starts, third, 2 * LANES, LANES)
-        return tops(last, 1, s, (mid[s], turn(q1, 3)))
+        mid2[s] = turn(q1, 2)
 
     for source in near_sources:
         for piece in range(last, len(pieces)):
@@ -456,10 +456,13 @@
     lax.fori_loop(0, n_seq, from_far, 0)
     for source in far_sources:
         wait_rows(last + 1, source)
-    lax.fori_loop(0, n_seq, from_far_tile, 0)
+    for s in range(n_seq):
+        from_far_tile(s, 0)
     for source in far_sources:
         wait_rows(last + 2, source)
-    found = [finish(s) for s in range(n_seq)]
+    for s in range(n_seq):
+        finish(s)
+    found = [tops(last, 1, s, (mid[s], mid2[s])) for s in range(n_seq)]
     keep(last, 1, [functools.reduce(jnp.maximum, tops_of) for tops_of in zip(*found)])
 
     top = jnp.max(jnp.max(macc[...], axis=1), axis=1, keepdims=True) * HEAD ** (-0.5)
@@ -495,7 +498,8 @@
 
 
 def scale_kernel(
-    n_sec, table, q_ref, k_ref, ratio_ref, q_out, k_out, q_buf, k_buf, q_row, k_row, q_sem, k_sem
+    n_sec, table, q_ref, k_ref, ratio_out, q_out, k_out, q_buf, k_buf, q_row, k_row, ratio_ref,
+    q_sem, k_sem, ratio_sem,
 ):
     group = table.shape[1]
     n_group, n_pair = q_ref.shape[1] // (group * HEAD), group // 2
@@ -549,9 +553,12 @@
             line = line + jnp.sum(jnp.where(here, values, 0.0), axis=0, keepdims=True)
         ratio_ref[layer:layer + 1, :] = line[:, :ratio_ref.shape[1]] / clip_threshold
 
+    ratio_copy = pltpu.make_async_copy(ratio_ref, ratio_out, ratio_sem)
+    ratio_copy.start()
     for i in range(n_chunk):
         block(q_buf, q_out, q_sem, i)[1].wait()
         block(k_buf, k_out, k_sem, i)[1].wait()
+    ratio_copy.wait()
 
 
 def exchanged(sizes, q_latent, kv_latent, segment_ids, q_weight, k_weight):
@@ -580,7 +587,8 @@
             pltpu.VMEM((group, LANES), jnp.float32),
             pltpu.VMEM((n_dp, length, 2 * HEAD), jnp.float32),
             pltpu.VMEM((n_dp, length, LANES), bf16),
-            pltpu.VMEM((6, length, LANES), jnp.float32),
+            pltpu.VMEM((n_dp, length, LANES), bf16),
+            pltpu.VMEM((4, length, LANES), jnp.float32),
             *[pltpu.SemaphoreType.REGULAR] * 4,
             dma,
             dma((n_dp, 2, 2)),
@@ -619,15 +627,16 @@
             jax.ShapeDtypeStruct(k_weight.shape[1:], bf16),
         ),
         in_specs=[pl.BlockSpec(memory_space=pltpu.VMEM)] * 3,
-        out_specs=[pl.BlockSpec(memory_space=pltpu.VMEM)]
-        + [pl.BlockSpec(memory_space=pltpu.HBM)] * 2,
+        out_specs=[pl.BlockSpec(memory_space=pltpu.HBM)] * 3,
         scratch_shapes=[
             pltpu.VMEM(q_weight.shape[1:], bf16),
             pltpu.VMEM(k_weight.shape[1:], bf16),
             pltpu.VMEM((1, q_weight.shape[2]), jnp.float32),
             pltpu.VMEM((1, k_weight.shape[2]), jnp.float32),
+            pltpu.VMEM((n_sec, heads), jnp.float32),
             dma((8,)),
             dma((8,)),
+            dma,
         ],
         compiler_params=pltpu.CompilerParams(vmem_limit_bytes=24 * 1024 * 1024),
         cost_estimate=pl.CostEstimate(

time: 143 us -> 141 us (0.986)
  no operation moved by 1% of the time
where the time goes in v3:
time: 141 us
  Pallas kernels  141 us (100%)
    pallas_call x1, Pallas kernels, exchanged(): pl.pallas_call(functools.partial(maxima_kernel, n_sec), out_shape=jax.Sha...  137 us
    pallas_call x1, Pallas kernels, exchanged(): pl.pallas_call(functools.partial(scale_kernel, n_sec), out_shape=(jax.Sha...  3.77 us

profile of v3, /device:TPU:0, one launch (start us, length us, event | category | flops | bytes accessed | tf_op | source)
XLA Modules:
  0.0 141.3 jit_solution(1902079496826651924)
XLA Ops:
  0.6 0.0 copy-start
  0.6 0.0 copy-start.1
  0.7 136.8 %maxima.1.table = f32[16,8,128]{2,1,0:T(8,128)S(1)} custom-call(bf16[512,1536]{1,0:T(8,128)(2,1)} %bitcast.15, bf16[576,512]{1,0:T(8,128)(2,1)} %bitcast.16, s32[1,512]{1,0:T(1,128)} %bitcast.17, bf16[384,6144]{1,0:T(8,128)(2,1)} %bitcast.9, bf16[512,4096]{1,0:T(8,128)(2,1)} %bitcast.11, f32[4,512,128]{2,1,0:T(8,128)} %constant.2.clone.tab_hbm), custom_call_target="tpu_custom_call" | custom-call | flops 15032385536 | bytes 4718592 | tf_op jit(solution)/shard_map/maxima/pallas_call | solution.py:573
  137.5 0.0 copy-done
  137.5 0.0 copy-done.1
  137.5 3.8 %scale.1 = (f32[4,32]{1,0:T(4,128)}, bf16[384,6144]{1,0:T(8,128)(2,1)}, bf16[512,4096]{1,0:T(8,128)(2,1)}) custom-call(f32[16,8,128]{2,1,0:T(8,128)S(1)} %maxima.1.table, bf16[384,6144]{1,0:T(8,128)(2,1)S(1)} %bitcast.10, bf16[512,4096]{1,0:T(8,128)(2,1)S(1)} %bitcast.12), custom_call_target="tpu_custom_call" | custom-call | flops 2359296 | bytes 18874368 | tf_op jit(solution)/shard_map/scale/pallas_call | solution.py:622
Async XLA Ops:
  0.6 136.8 %copy-start = (bf16[1,384,6144]{2,1,0:T(8,128)(2,1)S(1)}, bf16[1,384,6144]{2,1,0:T(8,128)(2,1)}, u32[]{:S(2)}) copy-start(bf16[1,384,6144]{2,1,0:T(8,128)(2,1)} %param.9) | copy-start | bytes 14155780
  0.6 136.8 %copy-start.1 = (bf16[1,512,4096]{2,1,0:T(8,128)(2,1)S(1)}, bf16[1,512,4096]{2,1,0:T(8,128)(2,1)}, u32[]{:S(2)}) copy-start(bf16[1,512,4096]{2,1,0:T(8,128)(2,1)} %param.10) | copy-start | bytes 12582916

commit v4 on v3

--- a/solution.py
+++ b/solution.py
@@ -145,8 +145,7 @@
 
     @pl.when(inner)
     def _():
-        for there in both_cores:
-            signal(barrier, {"dp": mid_z, "section": there})
+        signal(barrier, {"dp": mid_z})
         for there in both_cores:
             signal(barrier, {"dp": outer_z, "section": there})
 
@@ -257,7 +256,7 @@
     def wait_rows(piece, source):
         ready(rows_of(piece, source), w_recv.at[piece, source])
 
-    pl.semaphore_wait(barrier, jnp.where(inner, 2, 2 + len(side_peers)))
+    pl.semaphore_wait(barrier, jnp.where(inner, 1, 2 + len(side_peers)))
 
     @pl.when(inner & jnp.logical_not(primary))
     def _():

time: 141 us -> 141 us (level)
  no operation moved by 1% of the time
where the time goes in v4:
time: 141 us
  Pallas kernels  140 us (99%)
    pallas_call x1, Pallas kernels, exchanged(): pl.pallas_call(functools.partial(maxima_kernel, n_sec), out_shape=jax.Sha...  136 us
    pallas_call x1, Pallas kernels, exchanged(): pl.pallas_call(functools.partial(scale_kernel, n_sec), out_shape=(jax.Sha...  3.77 us

profile of v4, /device:TPU:0, one launch (start us, length us, event | category | flops | bytes accessed | tf_op | source)
XLA Modules:
  0.0 140.7 jit_solution(7133254695542869776)
XLA Ops:
  0.6 0.0 copy-start
  0.6 0.0 copy-start.1
  0.7 136.2 %maxima.1.table = f32[16,8,128]{2,1,0:T(8,128)S(1)} custom-call(bf16[512,1536]{1,0:T(8,128)(2,1)} %bitcast.15, bf16[576,512]{1,0:T(8,128)(2,1)} %bitcast.16, s32[1,512]{1,0:T(1,128)} %bitcast.17, bf16[384,6144]{1,0:T(8,128)(2,1)} %bitcast.9, bf16[512,4096]{1,0:T(8,128)(2,1)} %bitcast.11, f32[4,512,128]{2,1,0:T(8,128)} %constant.2.clone.tab_hbm), custom_call_target="tpu_custom_call" | custom-call | flops 15032385536 | bytes 4718592 | tf_op jit(solution)/shard_map/maxima/pallas_call | solution.py:572
  136.9 0.0 copy-done
  136.9 0.0 copy-done.1
  136.9 3.8 %scale.1 = (f32[4,32]{1,0:T(4,128)}, bf16[384,6144]{1,0:T(8,128)(2,1)}, bf16[512,4096]{1,0:T(8,128)(2,1)}) custom-call(f32[16,8,128]{2,1,0:T(8,128)S(1)} %maxima.1.table, bf16[384,6144]{1,0:T(8,128)(2,1)S(1)} %bitcast.10, bf16[512,4096]{1,0:T(8,128)(2,1)S(1)} %bitcast.12), custom_call_target="tpu_custom_call" | custom-call | flops 2359296 | bytes 18874368 | tf_op jit(solution)/shard_map/scale/pallas_call | solution.py:621
Async XLA Ops:
  0.6 136.3 %copy-start = (bf16[1,384,6144]{2,1,0:T(8,128)(2,1)S(1)}, bf16[1,384,6144]{2,1,0:T(8,128)(2,1)}, u32[]{:S(2)}) copy-start(bf16[1,384,6144]{2,1,0:T(8,128)(2,1)} %param.9) | copy-start | bytes 14155780
  0.6 136.3 %copy-start.1 = (bf16[1,512,4096]{2,1,0:T(8,128)(2,1)S(1)}, bf16[1,512,4096]{2,1,0:T(8,128)(2,1)}, u32[]{:S(2)}) copy-start(bf16[1,512,4096]{2,1,0:T(8,128)(2,1)} %param.10) | copy-start | bytes 12582916
